TPU v7x, 256 devices: a whole 4x4x8 slice. The times are simulated.
256 devices in a mesh: ctx: 8 (over z), exp: 32 (over x, y, core).
Axes of the slice: x: 4, y: 4, z: 8, core: 2. Of those that a mesh axis runs over, the one named last changes fastest.
Arguments:
- q_latent: bfloat16 [128, 128, 512], P('exp'), may hold values from -7 to 7
- q_rope: bfloat16 [128, 64, 128], P('exp'), may hold values from -84 to 84
- cache_latent: bfloat16 [128, 4096, 512], P('exp', 'ctx'), may hold values from -6 to 6
- cache_rope: bfloat16 [128, 64, 4096], P('exp', None, 'ctx'), may hold values from -6 to 6
- lengths: int32 [128], P('exp'), may hold values from 1024 to 4096
- w_attn_out: bfloat16 [128, 512, 7168], P('ctx', None, 'exp'), may hold values from -0.1875 to 0.1875
- hidden_in: bfloat16 [128, 7168], P(None, 'exp'), may hold values from -6 to 6
- norm_gain: bfloat16 [7168], replicated, may hold values from 0.5 to 8
- w_gate: bfloat16 [32, 7168, 1024], P('exp', None, 'ctx'), may hold values from -0.0625 to 0.0625
- w_up: bfloat16 [32, 7168, 1024], P('exp', None, 'ctx'), may hold values from -0.0625 to 0.0625
- w_down: bfloat16 [32, 1024, 7168], P('exp', 'ctx'), may hold values from -0.1875 to 0.1875
- expert_ids: int32 [128, 8], replicated, may hold values from 0 to 31, all different within a row; in each aligned block of 128 rows (0 to 127, 128 to 255, ...) at most 64 rows name the same one
- gate_weights: float32 [128, 8], replicated, may hold values from 0.1 to 1
Outputs:
- layer_out: bfloat16 [128, 7168], P('exp', 'ctx')
Inputs may be any that keep to these rules, and one draw needn't show every extreme that they name: `expert_ids`: each row names 8 different experts; over all 128 rows no expert is named more than 64 times, a bound that some block reaches.
All inputs are finite; a program needn't handle non-finite values.
Results may differ from a plain program's by a relative error of at most 0.008.
Values may be sent and summed in bfloat16 or wider, within the bound.
A program may use at most 64 MiB of HBM per device.

v0:
```python
import math
import jax
import jax.numpy as jnp
from jax import lax
from jax.sharding import PartitionSpec as P

SOFTMAX_SCALE = 192.0 ** (-0.5)
MASKED = -1e30
EPSILON = 1e-06


def cut_along(array, dim, devices):
    before, after = (array.shape[:dim], array.shape[dim + 1 :])
    return jnp.moveaxis(array.reshape(*before, devices, -1, *after), dim, 0)


def summed_on_arrival(array, axis, dim):
    devices = lax.axis_size(axis)
    blocks = lax.all_to_all(cut_along(array, dim, devices), axis, 0, 0, tiled=True)
    return jnp.sum(blocks, axis=0)


def sent_together(arrays, axis, dim, along):
    widths = [math.prod(a.shape[along:]) for a in arrays]
    both = jnp.concatenate(
        [a.reshape(*a.shape[:along], w) for a, w in zip(arrays, widths)], axis=along
    )
    filled = summed_on_arrival(both, axis, dim)
    blocks = jnp.split(filled, [sum(widths[:k]) for k in range(1, len(widths))], axis=along)
    return tuple(
        (b.reshape(*filled.shape[:along], *a.shape[along:]) for a, b in zip(arrays, blocks))
    )


def copy_for_each(array, axis):
    copies = jnp.broadcast_to(array, (lax.axis_size(axis), *array.shape))
    return lax.all_to_all(copies, axis, split_axis=0, concat_axis=0, tiled=True)


def taken_together(array, axis):
    everything = copy_for_each(array, axis)
    return jnp.sum(everything, axis=0)


def slot_tables(expert_ids, gate_weights, experts, capacity):
    row_count, top_count = expert_ids.shape
    flat_ids = expert_ids.reshape(-1)
    one_hot = (flat_ids[:, None] == jnp.arange(experts, dtype=jnp.int32)[None, :]).astype(jnp.int32)
    before = jnp.cumsum(one_hot, axis=0) - one_hot
    slot_index = jnp.sum(before * one_hot, axis=1)
    target = flat_ids * capacity + slot_index
    owner_row = jnp.arange(row_count * top_count, dtype=jnp.int32) // top_count
    slot_row = jnp.full((experts * capacity,), row_count, jnp.int32).at[target].set(owner_row)
    slot_gate = (
        jnp.zeros((experts * capacity,), jnp.float32).at[target].set(gate_weights.reshape(-1))
    )
    return (slot_row, slot_gate)


def per_device(
    q_latent,
    q_rope,
    cache_latent,
    cache_rope,
    lengths,
    w_attn_out,
    hidden_in,
    norm_gain,
    w_gate,
    w_up,
    w_down,
    expert_ids,
    gate_weights,
):
    ctx_index = lax.axis_index("ctx")
    exp_index = lax.axis_index("exp")
    ctx_count = lax.axis_size("ctx")
    exp_count = lax.axis_size("exp")
    block_len = cache_latent.shape[1]
    positions = ctx_index * block_len + jnp.arange(block_len, dtype=jnp.int32)
    visible = positions[None, :] < lengths[:, None]
    scores = jnp.einsum("rhl,rpl->rhp", q_latent, cache_latent, preferred_element_type=jnp.float32)
    scores = (
        scores + jnp.einsum("rdh,rdp->rhp", q_rope, cache_rope, preferred_element_type=jnp.float32)
    ) * SOFTMAX_SCALE
    scores = jnp.where(visible[:, None, :], scores, MASKED)
    block_max = jnp.max(scores, axis=2)
    weights = jnp.where(visible[:, None, :], jnp.exp(scores - block_max[..., None]), 0.0)
    block_total = jnp.sum(weights, axis=2)
    block_value = jnp.einsum(
        "rhp,rpl->rhl",
        weights.astype(jnp.bfloat16),
        cache_latent,
        preferred_element_type=jnp.float32,
    )
    head_count = w_attn_out.shape[0]
    joint_max = lax.pmax(block_max, "ctx")
    rescale = jnp.exp(block_max - joint_max)
    share_total, share_value = sent_together(
        (block_total * rescale, block_value * rescale[..., None]), "ctx", 1, 2
    )
    attended = (share_value / share_total[..., None]).astype(jnp.bfloat16)
    latent_width = w_attn_out.shape[1]
    flat_weight = w_attn_out.reshape(head_count * latent_width, w_attn_out.shape[2])
    row_piece = lax.all_gather(attended, "exp", axis=0, tiled=True)
    partial_out = jnp.dot(
        row_piece.reshape(row_piece.shape[0], head_count * latent_width),
        flat_weight,
        preferred_element_type=jnp.float32,
    )
    hidden_state = hidden_in.astype(jnp.float32) + taken_together(partial_out, "ctx")
    row_count = hidden_in.shape[0]
    share_width = hidden_in.shape[1]
    model_width = share_width * exp_count
    column_width = model_width // ctx_count
    top_count = expert_ids.shape[1]
    local_experts = w_gate.shape[0]
    experts = exp_count * local_experts
    capacity = min(row_count, 2 * row_count * top_count // experts)
    slot_row, slot_gate = slot_tables(expert_ids, gate_weights, experts, capacity)
    rounded = hidden_state.astype(jnp.bfloat16)
    padded = jnp.concatenate([rounded, jnp.zeros((1, share_width), jnp.bfloat16)], axis=0)
    outbound = padded[slot_row].reshape(experts, capacity, share_width)
    values = lax.all_to_all(outbound, "exp", split_axis=0, concat_axis=2, tiled=True).astype(
        jnp.float32
    )
    mean_square = jnp.mean(values * values, axis=2, keepdims=True)
    normed = (values * lax.rsqrt(mean_square + EPSILON) * norm_gain.astype(jnp.float32)).astype(
        jnp.bfloat16
    )
    gate_part = jnp.einsum("end,edf->enf", normed, w_gate, preferred_element_type=jnp.float32)
    up_part = jnp.einsum("end,edf->enf", normed, w_up, preferred_element_type=jnp.float32)
    active = (jax.nn.silu(gate_part) * up_part).astype(jnp.bfloat16)
    expert_part = jnp.einsum("enf,efd->end", active, w_down, preferred_element_type=jnp.float32)
    local_rows = lax.dynamic_slice_in_dim(
        slot_row, exp_index * local_experts * capacity, local_experts * capacity
    )
    local_gates = lax.dynamic_slice_in_dim(
        slot_gate, exp_index * local_experts * capacity, local_experts * capacity
    )
    weighted = expert_part.reshape(local_experts * capacity, model_width) * local_gates[:, None]
    owner_block = exp_index * share_width // column_width
    offset = exp_index * share_width % column_width
    column_part = summed_on_arrival(weighted, "ctx", 1)
    summed = jax.ops.segment_sum(column_part, local_rows, num_segments=row_count)
    current = lax.dynamic_slice(summed, (0, offset), (row_count, share_width))
    residual = jnp.where(ctx_index == owner_block, hidden_state, 0.0)
    summed = lax.dynamic_update_slice(summed, current + residual, (0, offset))
    layer_out = summed_on_arrival(summed, "exp", 0)
    return layer_out.astype(jnp.bfloat16)


def solution(mesh):
    in_specs = (
        P("exp", None, None),
        P("exp", None, None),
        P("exp", "ctx", None),
        P("exp", None, "ctx"),
        P("exp"),
        P("ctx", None, "exp"),
        P(None, "exp"),
        P(),
        P("exp", None, "ctx"),
        P("exp", None, "ctx"),
        P("exp", "ctx", None),
        P(),
        P(),
    )
    out_specs = P("exp", "ctx")
    return jax.shard_map(
        per_device, mesh=mesh, in_specs=in_specs, out_specs=out_specs, check_vma=False
    )
```

profile of v0, /device:TPU:1, one launch (start us, length us, event | category | flops | bytes accessed | tf_op | source)
XLA Modules:
  0.0 277.0 jit_solution(6442682698349328505)
XLA Ops:
  6.5 0.9 broadcast_compare_fusion
  7.4 0.7 copy-done
  8.1 1.9 fusion.58
  10.5 17.3 %pmax.7 = f32[4,128]{1,0:T(4,128)S(1)} all-reduce(f32[4,128]{1,0:T(4,128)S(1)} %get-tuple-element.7), channel_id=1, replica_groups=mesh['ctx'=8,'exp'=32] {'ctx'}, use_global_device_ids=true, to_apply=%region_6.7 | all-reduce | flops 512 | bytes 4096 | tf_op jit(solution)/shard_map/pmax | solution.py:97
  28.1 1.6 convolution_multiply_fusion
  30.0 1.6 maximum_bitcast_fusion
  31.7 31.7 %all_to_all.29 = f32[8,4,16,513]{3,2,1,0:T(8,128)S(1)} all-to-all(f32[8,4,16,513]{3,2,1,0:T(8,128)S(1)} %maximum_bitcast_fusion), channel_id=1, replica_groups=mesh['ctx'=8,'exp'=32] {'ctx'}, dimensions={0} | all-to-all | bytes 2101248 | tf_op jit(solution)/shard_map/all_to_all | solution.py:19
  63.3 0.7 reduce_sum.68
  64.1 0.8 slice_reduce_fusion
  64.9 1.6 fusion.37
  66.6 51.4 %all-gather.2.cloned.1.call-done = bf16[128,16,512]{2,1,0:T(8,128)(2,1)} async-done(((bf16[4,16,512]{2,1,0:T(8,128)(2,1)}), bf16[128,16,512]{2,1,0:T(8,128)(2,1)}) %all-gather.2.cloned.1.call-update) | async-done | bytes 2097168 | tf_op jit(solution)/shard_map/all_gather | solution.py:105
  118.0 5.2 %fusion.11 = f32[128,224]{0,1:T(8,128)S(1)} fusion(bf16[16,512,224]{1,2,0:T(8,128)(2,1)} %param.18, bf16[128,16,512]{2,1,0:T(8,128)(2,1)} %all-gather.2.cloned.1.call-done), kind=kOutput, calls=%fused_computation.21 | convolution fusion | flops 469762048 | bytes 5881856 | tf_op jit(solution)/shard_map/dot_general | solution.py:106
  123.2 1.0 broadcast_in_dim.59
  124.2 6.7 %all-to-all-start.1 = ((f32[8,128,224]{1,2,0:T(8,128)}), f32[8,128,224]{1,2,0:T(8,128)S(1)}, u32[]{:S(2)}, u32[]{:S(2)}) async-start(f32[8,128,224]{1,2,0:T(8,128)} %broadcast_in_dim.59), calls=%async_computation.1 | async-start | bytes 1835008 | tf_op jit(solution)/shard_map/all_to_all | solution.py:37
  131.6 9.0 %reduce-window.6 = s32[32,8,128]{2,1,0:T(8,128)S(1)} reduce-window(s32[32,8,128]{2,1,0:T(8,128)S(1)} %fusion.38, s32[]{:T(128)} %constant.34.clone.1), window={size=1x1x128 pad=0_0x0_0x127_0}, to_apply=%region_0.1 | reduce-window | flops 4161536 | bytes 262148 | tf_op jit(solution)/shard_map/reduce-window
  141.1 4.3 %scatter_custom_fusion = s32[2048]{0:T(1024)S(1)} fusion(s32[1024]{0:T(1024)S(1)} %bitcast.76, s32[1024]{0:T(1024)S(1)} %add_select_fusion, s32[]{:T(128)} %constant.31.clone.1), kind=kCustom, calls=%fused_computation.66 | custom fusion | bytes 8196 | tf_op jit(solution)/shard_map/scatter | solution.py:53
  145.5 11.9 %all-to-all-done.1 = f32[8,128,224]{1,2,0:T(8,128)S(1)} async-done(((f32[8,128,224]{1,2,0:T(8,128)}), f32[8,128,224]{1,2,0:T(8,128)S(1)}, u32[]{:S(2)}, u32[]{:S(2)}) %all-to-all-start.1) | async-done | bytes 917536 | tf_op jit(solution)/shard_map/all_to_all | solution.py:37
  157.5 9.0 %gather_fusion = bf16[2048,224]{1,0:T(8,128)(2,1)} fusion(bf16[129,224]{1,0:T(8,128)(2,1)S(1)} %concatenate.14, s32[2048]{0:T(1024)S(1)} %fusion.46), kind=kCustom, calls=%fused_computation | custom fusion | bytes 1843200 | tf_op jit(solution)/shard_map/gather | solution.py:123
  166.5 5.6 %all-to-all-start.2 = ((bf16[32,64,224]{2,1,0:T(8,128)(2,1)}), bf16[32,64,224]{2,1,0:T(8,128)(2,1)S(1)}, u32[]{:S(2)}, u32[]{:S(2)}) async-start(bf16[32,64,224]{2,1,0:T(8,128)(2,1)} %bitcast.71), calls=%async_computation.2 | async-start | bytes 2097152 | tf_op jit(solution)/shard_map/all_to_all | solution.py:124
  172.4 4.5 %scatter_custom_fusion.1 = f32[2048]{0:T(1024)S(1)} fusion(s32[1024]{0:T(1024)S(1)} %bitcast.77, f32[1024]{0:T(1024)S(1)} %reshape.230, f32[]{:T(128)} %constant.28.clone.1), kind=kCustom, calls=%fused_computation.63 | custom fusion | bytes 8196 | tf_op jit(solution)/shard_map/scatter | solution.py:55
  176.9 3.9 %copy.72 = bf16[7168,128]{1,0:T(8,128)(2,1)} copy(bf16[7168,128]{0,1:T(8,128)(2,1)} %bitcast.72) | data formatting | bytes 3670016 | tf_op jit(solution)/shard_map/enf,efd->end/dot_general | solution.py:134
  180.9 8.1 %all-to-all-done.2 = bf16[32,64,224]{2,1,0:T(8,128)(2,1)S(1)} async-done(((bf16[32,64,224]{2,1,0:T(8,128)(2,1)}), bf16[32,64,224]{2,1,0:T(8,128)(2,1)S(1)}, u32[]{:S(2)}, u32[]{:S(2)}) %all-to-all-start.2) | async-done | bytes 917536 | tf_op jit(solution)/shard_map/all_to_all | solution.py:124
  189.7 1.6 copy.69
  191.3 2.6 convert_element_type.70
  193.9 2.0 fusion.7
  195.9 4.5 %multiply_bitcast_fusion = f32[8,64,896]{2,1,0:T(8,128)} fusion(bf16[8,896,128]{2,1,0:T(8,128)(2,1)} %bitcast.69, f32[64]{0:T(128)S(1)} %dynamic_slice.10, bf16[64,7168]{1,0:T(8,128)(2,1)S(1)} %convert_element_type.70, bf16[1,7168,128]{2,1,0:T(8,128)(2,1)} %param.22, f32[64,128]{1,0:T(8,128)S(1)} %fusion.7), kind=kOutput, calls=%fused_computation.15 | convolution fusion | flops 235388928 | bytes 6455552 | tf_op jit(solution)/shard_map/enf,efd->end/dot_general | solution.py:134
  200.4 4.3 %all-to-all-start.3 = ((f32[8,64,896]{2,1,0:T(8,128)}), f32[8,64,896]{2,1,0:T(8,128)}, u32[]{:S(2)}, u32[]{:S(2)}) async-start(f32[8,64,896]{2,1,0:T(8,128)} %multiply_bitcast_fusion), calls=%async_computation.3 | async-start | bytes 3670016 | tf_op jit(solution)/shard_map/all_to_all | solution.py:19
  204.8 43.0 %all-to-all-done.3 = f32[8,64,896]{2,1,0:T(8,128)} async-done(((f32[8,64,896]{2,1,0:T(8,128)}), f32[8,64,896]{2,1,0:T(8,128)}, u32[]{:S(2)}, u32[]{:S(2)}) %all-to-all-start.3) | async-done | bytes 1835040 | tf_op jit(solution)/shard_map/all_to_all | solution.py:19
  247.8 1.6 reduce_sum.71
  249.5 1.2 scatter_custom_fusion.2
  250.8 1.3 dynamic_update_slice.3
  252.2 17.2 %all_to_all.30 = f32[32,4,896]{2,1,0:T(4,128)S(1)} all-to-all(f32[32,4,896]{2,1,0:T(4,128)S(1)} %reshape.207), channel_id=1, replica_groups=mesh['ctx'=8,'exp'=32] {'exp'}, dimensions={0} | all-to-all | bytes 917504 | tf_op jit(solution)/shard_map/all_to_all | solution.py:19
  (54 shorter events, 4.5 us)
Async XLA Ops:
  6.5 1.6 copy-start
  6.5 111.4 %all-gather.2.cloned.1.call-start = ((), (), s32[]{:S(2)}) async-start(), calls=%async_computation.5 | async-start | bytes 2162688 | tf_op jit(solution)/shard_map/all_gather | solution.py:105
  8.1 1.9 copy-start.1
  8.1 1.9 copy-start.2
  123.2 7.7 %copy-start.4 = (s32[128,8]{0,1:T(8,128)S(1)}, s32[128,8]{0,1:T(8,128)}, u32[]{:S(2)}) copy-start(s32[128,8]{0,1:T(8,128)} %param.24) | copy-start | bytes 12292
  123.2 8.2 %copy-start.3 = (bf16[128,224]{0,1:T(8,128)(2,1)S(1)}, bf16[128,224]{0,1:T(8,128)(2,1)}, u32[]{:S(2)}) copy-start(bf16[128,224]{0,1:T(8,128)(2,1)} %param.19) | copy-start | bytes 172036
  124.2 33.1 %all-to-all-start.1 = ((f32[8,128,224]{1,2,0:T(8,128)}), f32[8,128,224]{1,2,0:T(8,128)S(1)}, u32[]{:S(2)}, u32[]{:S(2)}) async-start(f32[8,128,224]{1,2,0:T(8,128)} %broadcast_in_dim.59), calls=%async_computation.1 | async-start | bytes 1835008 | tf_op jit(solution)/shard_map/all_to_all | solution.py:37
  166.5 5.6 %copy-start.5 = (bf16[7168]{0:T(1024)(128)(2,1)S(1)}, bf16[7168]{0:T(1024)(128)(2,1)}, u32[]{:S(2)}) copy-start(bf16[7168]{0:T(1024)(128)(2,1)} %param.20) | copy-start | bytes 43012
  166.5 5.7 %copy-start.6 = (f32[128,8]{0,1:T(8,128)S(1)}, f32[128,8]{0,1:T(8,128)}, u32[]{:S(2)}) copy-start(f32[128,8]{0,1:T(8,128)} %param.25) | copy-start | bytes 12292
  166.5 22.5 %all-to-all-start.2 = ((bf16[32,64,224]{2,1,0:T(8,128)(2,1)}), bf16[32,64,224]{2,1,0:T(8,128)(2,1)S(1)}, u32[]{:S(2)}, u32[]{:S(2)}) async-start(bf16[32,64,224]{2,1,0:T(8,128)(2,1)} %bitcast.71), calls=%async_computation.2 | async-start | bytes 2097152 | tf_op jit(solution)/shard_map/all_to_all | solution.py:124
  200.4 47.5 %all-to-all-start.3 = ((f32[8,64,896]{2,1,0:T(8,128)}), f32[8,64,896]{2,1,0:T(8,128)}, u32[]{:S(2)}, u32[]{:S(2)}) async-start(f32[8,64,896]{2,1,0:T(8,128)} %multiply_bitcast_fusion), calls=%async_computation.3 | async-start | bytes 3670016 | tf_op jit(solution)/shard_map/all_to_all | solution.py:19
Sparse Core Ops, SparseCore 0:
  66.7 51.2 all-gather.1
where the time goes:
time: 278 us; the launch traced here: 277 us
  waiting for transfers between devices  114 us (41%)
  blocking collectives  66.1 us (24%)
  local copies, waits for them, and re-layouts  31.7 us (11%)
  other arithmetic  18.8 us (7%)
  starting transfers between devices  16.6 us (6%)
  matrix products  15.6 us (6%)
  between operations  13.7 us (5%)
    all_gather x1, waiting for transfers between devices, per_device(): row_piece = lax.all_gather(attended, 'exp', axis=0, tiled=True)  51.4 us
    all_to_all x2, blocking collectives, summed_on_arrival(): lax.all_to_all(cut_along(array, dim, devices), axis, 0, 0, tiled=True)  48.9 us
    all_to_all x1, waiting for transfers between devices, summed_on_arrival(): lax.all_to_all(cut_along(array, dim, devices), axis, 0, 0, tiled=True)  43 us
    pmax x1, blocking collectives, per_device(): joint_max = lax.pmax(block_max, 'ctx')  17.3 us
    all_to_all x1, waiting for transfers between devices, copy_for_each(): return lax.all_to_all(copies, axis, split_axis=0, concat_axis=0, tiled=True)  11.9 us
    another operation x3, other arithmetic  9.15 us
    gather x1, local copies, waits for them, and re-layouts, per_device(): outbound = padded[slot_row].reshape(experts, capacity, share_width)  9 us
    all_to_all x1, waiting for transfers between devices, per_device(): lax.all_to_all(outbound, 'exp', split_axis=0, concat_axis=2, tiled=True)  8.11 us
  transfers between devices with their start and end apart: 4, of which 4 were waited for; matrix products, arithmetic and copies ran while one was open for 8% of the time, Pallas kernels for 0%

commit v1 on v0

--- a/solution.py
+++ b/solution.py
@@ -72,6 +72,18 @@
     expert_ids,
     gate_weights,
 ):
+
+    def post_object(body, dev_axis):
+        axis_total = lax.axis_size(dev_axis)
+        piece_now = lax.all_to_all(
+            jnp.tile(body, [axis_total if nth == 0 else 1 for nth in range(body.ndim)]),
+            axis_name=dev_axis,
+            split_axis=0,
+            concat_axis=0,
+            tiled=True,
+        )
+        return piece_now
+
     ctx_index = lax.axis_index("ctx")
     exp_index = lax.axis_index("exp")
     ctx_count = lax.axis_size("ctx")
@@ -102,7 +114,7 @@
     attended = (share_value / share_total[..., None]).astype(jnp.bfloat16)
     latent_width = w_attn_out.shape[1]
     flat_weight = w_attn_out.reshape(head_count * latent_width, w_attn_out.shape[2])
-    row_piece = lax.all_gather(attended, "exp", axis=0, tiled=True)
+    row_piece = post_object(attended, "exp")
     partial_out = jnp.dot(
         row_piece.reshape(row_piece.shape[0], head_count * latent_width),
         flat_weight,

time: 278 us -> 247 us (0.89)
  waiting for transfers between devices: 114 us -> 63.1 us
  blocking collectives: 66.1 us -> 108 us
  between operations: 13.7 us -> 0.34 us
  starting transfers between devices: 16.6 us -> 12 us
  matrix products: 15.6 us -> 12.8 us
    all_gather x1 -> x0, waiting for transfers between devices: 51.4 us -> none  [per_device(): row_piece = lax.all_gather(attended, 'exp', axis=0, tiled=True)]
    all_to_all x0 -> x1, blocking collectives: none -> 41.9 us  [post_object(): lax.all_to_all(jnp.tile(body, [axis_total if nth == 0 else 1 for nth in r...]
    all_to_all x1, starting transfers between devices: 6.73 us -> 3.55 us  [copy_for_each(): return lax.all_to_all(copies, axis, split_axis=0, concat_axis=0, tiled=True)]
  transfers between devices with their start and end apart: 4 -> 3, of which waited for: 4 -> 3; matrix products, arithmetic and copies ran while one was open for 8% -> 9% of each run, Pallas kernels for 0% -> 0%
where the time goes in v1:
time: 247 us; the launch traced here: 246 us
  blocking collectives  108 us (44%)
  waiting for transfers between devices  63.1 us (26%)
  local copies, waits for them, and re-layouts  31.9 us (13%)
  other arithmetic  18.2 us (7%)
  matrix products  12.8 us (5%)
  starting transfers between devices  12 us (5%)
    all_to_all x2, blocking collectives, summed_on_arrival(): lax.all_to_all(cut_along(array, dim, devices), axis, 0, 0, tiled=True)  48.9 us
    all_to_all x1, waiting for transfers between devices, summed_on_arrival(): lax.all_to_all(cut_along(array, dim, devices), axis, 0, 0, tiled=True)  43.1 us
    all_to_all x1, blocking collectives, post_object(): lax.all_to_all(jnp.tile(body, [axis_total if nth == 0 else 1 for nth in r...  41.9 us
    pmax x1, blocking collectives, per_device(): joint_max = lax.pmax(block_max, 'ctx')  17.3 us
    all_to_all x1, waiting for transfers between devices, copy_for_each(): return lax.all_to_all(copies, axis, split_axis=0, concat_axis=0, tiled=True)  11.8 us
    another operation x3, other arithmetic  9.14 us
    gather x1, local copies, waits for them, and re-layouts, per_device(): outbound = padded[slot_row].reshape(experts, capacity, share_width)  9 us
    all_to_all x1, waiting for transfers between devices, per_device(): lax.all_to_all(outbound, 'exp', split_axis=0, concat_axis=2, tiled=True)  8.21 us
  transfers between devices with their start and end apart: 3, of which 3 were waited for; matrix products, arithmetic and copies ran while one was open for 9% of the time, Pallas kernels for 0%

profile of v1, /device:TPU:1, one launch (start us, length us, event | category | flops | bytes accessed | tf_op | source)
XLA Modules:
  0.0 246.5 jit_solution(12845880481138988821)
XLA Ops:
  0.0 0.9 broadcast_compare_fusion
  0.9 0.7 copy-done
  1.6 1.8 fusion.58
  3.9 17.3 %pmax.7 = f32[4,128]{1,0:T(4,128)S(1)} all-reduce(f32[4,128]{1,0:T(4,128)S(1)} %get-tuple-element.7), channel_id=1, replica_groups=mesh['ctx'=8,'exp'=32] {'ctx'}, use_global_device_ids=true, to_apply=%region_6.7 | all-reduce | flops 512 | bytes 4096 | tf_op jit(solution)/shard_map/pmax | solution.py:109
  21.5 1.6 convolution_multiply_fusion
  23.5 1.6 maximum_bitcast_fusion
  25.1 31.7 %all_to_all.34 = f32[8,4,16,513]{3,2,1,0:T(8,128)S(1)} all-to-all(f32[8,4,16,513]{3,2,1,0:T(8,128)S(1)} %maximum_bitcast_fusion), channel_id=1, replica_groups=mesh['ctx'=8,'exp'=32] {'ctx'}, dimensions={0} | all-to-all | bytes 2101248 | tf_op jit(solution)/shard_map/all_to_all | solution.py:19
  56.7 0.7 reduce_sum.68
  57.5 0.8 slice_reduce_fusion
  58.3 1.0 fusion.37
  59.6 41.9 %all_to_all.35 = bf16[128,16,512]{2,1,0:T(8,128)(2,1)S(1)} all-to-all(bf16[128,16,512]{2,1,0:T(8,128)(2,1)S(1)} %bitcast.68), channel_id=1, replica_groups=mesh['ctx'=8,'exp'=32] {'exp'}, dimensions={0} | all-to-all | bytes 4194304 | tf_op jit(solution)/shard_map/all_to_all | solution.py:78
  101.5 2.6 %fusion.11 = f32[128,224]{0,1:T(8,128)S(1)} fusion(bf16[16,512,224]{1,2,0:T(8,128)(2,1)S(1)} %copy-done.7, bf16[128,16,512]{2,1,0:T(8,128)(2,1)S(1)} %all_to_all.35), kind=kOutput, calls=%fused_computation.21 | convolution fusion | flops 469762048 | bytes 5881856 | tf_op jit(solution)/shard_map/dot_general | solution.py:118
  104.1 1.0 broadcast_in_dim.59
  105.1 3.6 %all-to-all-start.2 = ((f32[8,128,224]{1,2,0:T(8,128)}), f32[8,128,224]{1,2,0:T(8,128)S(1)}, u32[]{:S(2)}, u32[]{:S(2)}) async-start(f32[8,128,224]{1,2,0:T(8,128)} %broadcast_in_dim.59), calls=%async_computation.2 | async-start | bytes 1835008 | tf_op jit(solution)/shard_map/all_to_all | solution.py:37
  109.1 9.0 %reduce-window.6 = s32[32,8,128]{2,1,0:T(8,128)S(1)} reduce-window(s32[32,8,128]{2,1,0:T(8,128)S(1)} %fusion.38, s32[]{:T(128)} %constant.34.clone.1), window={size=1x1x128 pad=0_0x0_0x127_0}, to_apply=%region_0.1 | reduce-window | flops 4161536 | bytes 262148 | tf_op jit(solution)/shard_map/reduce-window
  118.8 4.3 %scatter_custom_fusion = s32[2048]{0:T(1024)S(1)} fusion(s32[1024]{0:T(1024)S(1)} %bitcast.76, s32[1024]{0:T(1024)S(1)} %add_select_fusion, s32[]{:T(128)} %constant.31.clone.1), kind=kCustom, calls=%fused_computation.66 | custom fusion | bytes 8196 | tf_op jit(solution)/shard_map/scatter | solution.py:53
  123.2 11.8 %all-to-all-done.2 = f32[8,128,224]{1,2,0:T(8,128)S(1)} async-done(((f32[8,128,224]{1,2,0:T(8,128)}), f32[8,128,224]{1,2,0:T(8,128)S(1)}, u32[]{:S(2)}, u32[]{:S(2)}) %all-to-all-start.2) | async-done | bytes 917536 | tf_op jit(solution)/shard_map/all_to_all | solution.py:37
  135.2 9.0 %gather_fusion = bf16[2048,224]{1,0:T(8,128)(2,1)} fusion(bf16[129,224]{1,0:T(8,128)(2,1)S(1)} %concatenate.14, s32[2048]{0:T(1024)S(1)} %fusion.46), kind=kCustom, calls=%fused_computation | custom fusion | bytes 1843200 | tf_op jit(solution)/shard_map/gather | solution.py:135
  144.2 4.2 %all-to-all-start.3 = ((bf16[32,64,224]{2,1,0:T(8,128)(2,1)}), bf16[32,64,224]{2,1,0:T(8,128)(2,1)S(1)}, u32[]{:S(2)}, u32[]{:S(2)}) async-start(bf16[32,64,224]{2,1,0:T(8,128)(2,1)} %bitcast.71), calls=%async_computation.3 | async-start | bytes 2097152 | tf_op jit(solution)/shard_map/all_to_all | solution.py:136
  148.6 4.5 %scatter_custom_fusion.1 = f32[2048]{0:T(1024)S(1)} fusion(s32[1024]{0:T(1024)S(1)} %bitcast.77, f32[1024]{0:T(1024)S(1)} %reshape.234, f32[]{:T(128)} %constant.28.clone.1), kind=kCustom, calls=%fused_computation.63 | custom fusion | bytes 8196 | tf_op jit(solution)/shard_map/scatter | solution.py:55
  153.2 3.9 %copy.70 = bf16[7168,128]{1,0:T(8,128)(2,1)} copy(bf16[7168,128]{0,1:T(8,128)(2,1)} %bitcast.72) | data formatting | bytes 3670016 | tf_op jit(solution)/shard_map/enf,efd->end/dot_general | solution.py:146
  157.1 8.2 %all-to-all-done.3 = bf16[32,64,224]{2,1,0:T(8,128)(2,1)S(1)} async-done(((bf16[32,64,224]{2,1,0:T(8,128)(2,1)}), bf16[32,64,224]{2,1,0:T(8,128)(2,1)S(1)}, u32[]{:S(2)}, u32[]{:S(2)}) %all-to-all-start.3) | async-done | bytes 917536 | tf_op jit(solution)/shard_map/all_to_all | solution.py:136
  166.1 1.6 copy.67
  167.6 2.6 %convert_element_type.70 = bf16[64,7168]{1,0:T(8,128)(2,1)S(1)} reshape(bf16[1,64,32,224]{3,2,1,0:T(8,128)(2,1)} %copy.67) | data formatting | bytes 1835008 | tf_op jit(solution)/shard_map/convert_element_type | solution.py:140
  170.3 2.0 fusion.7
  172.2 4.5 %multiply_bitcast_fusion = f32[8,64,896]{2,1,0:T(8,128)} fusion(bf16[8,896,128]{2,1,0:T(8,128)(2,1)} %bitcast.69, f32[64]{0:T(128)S(1)} %dynamic_slice.10, bf16[64,7168]{1,0:T(8,128)(2,1)S(1)} %convert_element_type.70, bf16[1,7168,128]{2,1,0:T(8,128)(2,1)} %param.22, f32[64,128]{1,0:T(8,128)S(1)} %fusion.7), kind=kOutput, calls=%fused_computation.15 | convolution fusion | flops 235388928 | bytes 6455552 | tf_op jit(solution)/shard_map/enf,efd->end/dot_general | solution.py:146
  176.7 4.3 %all-to-all-start.4 = ((f32[8,64,896]{2,1,0:T(8,128)}), f32[8,64,896]{2,1,0:T(8,128)}, u32[]{:S(2)}, u32[]{:S(2)}) async-start(f32[8,64,896]{2,1,0:T(8,128)} %multiply_bitcast_fusion), calls=%async_computation.4 | async-start | bytes 3670016 | tf_op jit(solution)/shard_map/all_to_all | solution.py:19
  181.1 43.1 %all-to-all-done.4 = f32[8,64,896]{2,1,0:T(8,128)} async-done(((f32[8,64,896]{2,1,0:T(8,128)}), f32[8,64,896]{2,1,0:T(8,128)}, u32[]{:S(2)}, u32[]{:S(2)}) %all-to-all-start.4) | async-done | bytes 1835040 | tf_op jit(solution)/shard_map/all_to_all | solution.py:19
  224.2 1.6 reduce_sum.71
  225.8 1.2 scatter_custom_fusion.2
  227.1 1.3 dynamic_update_slice.3
  228.5 17.2 %all_to_all.36 = f32[32,4,896]{2,1,0:T(4,128)S(1)} all-to-all(f32[32,4,896]{2,1,0:T(4,128)S(1)} %reshape.211), channel_id=1, replica_groups=mesh['ctx'=8,'exp'=32] {'exp'}, dimensions={0} | all-to-all | bytes 917504 | tf_op jit(solution)/shard_map/all_to_all | solution.py:19
  (55 shorter events, 4.7 us)
Async XLA Ops:
  0.0 1.6 copy-start
  0.0 3.5 %copy-start.2 = (bf16[4,64,128]{2,1,0:T(8,128)(2,1)S(1)}, bf16[4,64,128]{2,1,0:T(8,128)(2,1)}, u32[]{:S(2)}) copy-start(bf16[4,64,128]{2,1,0:T(8,128)(2,1)} %param.14) | copy-start | bytes 196612
  0.0 3.5 %copy-start.1 = (bf16[4,64,512]{2,1,0:T(8,128)(2,1)S(1)}, bf16[4,64,512]{2,1,0:T(8,128)(2,1)}, u32[]{:S(2)}) copy-start(bf16[4,64,512]{2,1,0:T(8,128)(2,1)} %param.16) | copy-start | bytes 786436
  59.6 41.9 %copy-start.7 = (bf16[16,512,224]{1,2,0:T(8,128)(2,1)S(1)}, bf16[16,512,224]{1,2,0:T(8,128)(2,1)}, u32[]{:S(2)}) copy-start(bf16[16,512,224]{1,2,0:T(8,128)(2,1)} %param.18) | copy-start | bytes 11010052
  104.1 4.6 %copy-start.4 = (s32[128,8]{0,1:T(8,128)S(1)}, s32[128,8]{0,1:T(8,128)}, u32[]{:S(2)}) copy-start(s32[128,8]{0,1:T(8,128)} %param.24) | copy-start | bytes 12292
  104.1 4.9 %copy-start.3 = (bf16[128,224]{0,1:T(8,128)(2,1)S(1)}, bf16[128,224]{0,1:T(8,128)(2,1)}, u32[]{:S(2)}) copy-start(bf16[128,224]{0,1:T(8,128)(2,1)} %param.19) | copy-start | bytes 172036
  105.1 29.9 %all-to-all-start.2 = ((f32[8,128,224]{1,2,0:T(8,128)}), f32[8,128,224]{1,2,0:T(8,128)S(1)}, u32[]{:S(2)}, u32[]{:S(2)}) async-start(f32[8,128,224]{1,2,0:T(8,128)} %broadcast_in_dim.59), calls=%async_computation.2 | async-start | bytes 1835008 | tf_op jit(solution)/shard_map/all_to_all | solution.py:37
  144.2 4.2 %copy-start.5 = (bf16[7168]{0:T(1024)(128)(2,1)S(1)}, bf16[7168]{0:T(1024)(128)(2,1)}, u32[]{:S(2)}) copy-start(bf16[7168]{0:T(1024)(128)(2,1)} %param.20) | copy-start | bytes 43012
  144.2 4.3 %copy-start.6 = (f32[128,8]{0,1:T(8,128)S(1)}, f32[128,8]{0,1:T(8,128)}, u32[]{:S(2)}) copy-start(f32[128,8]{0,1:T(8,128)} %param.25) | copy-start | bytes 12292
  144.2 21.2 %all-to-all-start.3 = ((bf16[32,64,224]{2,1,0:T(8,128)(2,1)}), bf16[32,64,224]{2,1,0:T(8,128)(2,1)S(1)}, u32[]{:S(2)}, u32[]{:S(2)}) async-start(bf16[32,64,224]{2,1,0:T(8,128)(2,1)} %bitcast.71), calls=%async_computation.3 | async-start | bytes 2097152 | tf_op jit(solution)/shard_map/all_to_all | solution.py:136
  176.7 47.5 %all-to-all-start.4 = ((f32[8,64,896]{2,1,0:T(8,128)}), f32[8,64,896]{2,1,0:T(8,128)}, u32[]{:S(2)}, u32[]{:S(2)}) async-start(f32[8,64,896]{2,1,0:T(8,128)} %multiply_bitcast_fusion), calls=%async_computation.4 | async-start | bytes 3670016 | tf_op jit(solution)/shard_map/all_to_all | solution.py:19
